TPU v7x, 128 devices: a whole 4x4x4 slice. The times are simulated.
128 devices in a mesh: freq: 4 (over x), shot: 32 (over y, z, core).
Axes of the slice: x: 4, y: 4, z: 4, core: 2. Of those that a mesh axis runs over, the one named last changes fastest.
Arguments:
- traces: bfloat16 [2, 4, 3072, 3072], P(None, 'freq', 'shot'), may hold values from -40 to 40, as said below
Outputs:
- multiples: bfloat16 [2, 4, 3072, 3072], P(None, 'freq', 'shot')
- primaries: bfloat16 [2, 4, 3072, 3072], P(None, 'freq', 'shot')
Inputs may be any that keep to these rules, and one draw needn't show every extreme that they name: `traces`: finite recorded data.
All inputs are finite; a program needn't handle non-finite values.
Results may differ from a plain program's by a relative error of at most 0.0005.
Values may be sent and summed in bfloat16 or wider, within the bound.
A program may use at most 192 MiB of HBM per device.

v0:
```python
import math

import jax
import jax.numpy as jnp
from jax import lax
from jax.sharding import PartitionSpec as P

epsilon = 1e-06


def from_everyone(shard, axis):
    size = lax.axis_size(axis)
    return lax.all_to_all(
        jnp.broadcast_to(shard[None], (size, *shard.shape)), axis, 0, 0, tiled=True
    )


def taken_together(shard, axis):
    return from_everyone(shard, axis).sum(axis=0)


def together(arrays, axis):
    line, at, done = (jnp.concatenate([a.reshape(-1) for a in arrays]), 0, [])
    subtotal = taken_together(line, axis)
    for a in arrays:
        done.append(subtotal[at : at + a.size].reshape(a.shape))
        at += a.size
    return tuple(done)


def complex_product(left_re, left_im, right):
    left_block = jnp.stack(
        [jnp.concatenate([left_re, -left_im], axis=2), jnp.concatenate([left_im, left_re], axis=2)]
    )
    right_block = jnp.concatenate([right[0], right[1]], axis=1)
    return jnp.einsum("cfik,fkn->cfin", left_block, right_block, preferred_element_type=jnp.float32)


def per_device(traces):
    matrix_order = traces.shape[3]
    bands = traces.shape[1]
    factor = 1.0 / math.sqrt(matrix_order)
    real_part = traces[0]
    imag_part = traces[1]
    whole = lax.all_gather(traces, "shot", axis=2, tiled=True)
    products = complex_product(real_part, imag_part, whole)
    mult_re = products[0] * factor
    mult_im = products[1] * factor
    data_re = traces[0].astype(jnp.float32)
    data_im = traces[1].astype(jnp.float32)
    partial_sums = (
        jnp.sum(mult_re * data_re + mult_im * data_im),
        jnp.sum(mult_re * data_im - mult_im * data_re),
        jnp.sum(mult_re * mult_re + mult_im * mult_im),
    )
    group_sums = together((partial_sums[0], partial_sums[1], partial_sums[2]), "shot")
    num_re, num_im, denom = together((group_sums[0], group_sums[1], group_sums[2]), "freq")
    total_count = float(bands * lax.axis_size("freq") * matrix_order * matrix_order)
    scaled_den = denom / total_count + epsilon
    fit_re = num_re / total_count / scaled_den
    fit_im = num_im / total_count / scaled_den
    prim_re = data_re - (fit_re * mult_re - fit_im * mult_im)
    prim_im = data_im - (fit_re * mult_im + fit_im * mult_re)
    multiples = jnp.stack([mult_re, mult_im]).astype(jnp.bfloat16)
    primaries = jnp.stack([prim_re, prim_im]).astype(jnp.bfloat16)
    return (multiples, primaries)


def solution(mesh):
    placed = (P(None, "freq", "shot", None),)
    return jax.shard_map(
        per_device,
        mesh=mesh,
        in_specs=placed,
        out_specs=(P(None, "freq", "shot", None), P(None, "freq", "shot", None)),
        check_vma=False,
    )
```

profile of v0, /device:TPU:1, one launch (start us, length us, event | category | flops | bytes accessed | tf_op | source)
XLA Modules:
  0.0 216.3 jit_solution(2821966199335791309)
XLA Ops:
  7.2 0.0 copy-start
  7.2 0.0 all-gather.2.cloned.1.call-start
  7.2 0.7 all-gather.2.cloned.1.call-update
  7.9 0.5 copy-done
  8.5 0.1 slice_bitcast_fusion.2
  8.6 1.6 maximum_bitcast_fusion.6
  10.1 128.5 %all-gather.2.cloned.1.call-done = bf16[2,1,3072,3072]{3,2,1,0:T(8,128)(2,1)} async-done(((bf16[2,1,96,3072]{3,2,1,0:T(8,128)(2,1)}), bf16[2,1,3072,3072]{3,2,1,0:T(8,128)(2,1)}) %all-gather.2.cloned.1.call-update) | async-done | bytes 37748752 | tf_op jit(solution)/shard_map/all_gather | solution.py:45
  138.7 25.2 %slice_bitcast_fusion.1 = (bf16[1,3072,3072]{2,1,0:T(8,128)(2,1)}, bf16[1,3072,3072]{2,1,0:T(8,128)(2,1)}) fusion(bf16[2,1,3072,3072]{3,2,1,0:T(8,128)(2,1)} %all-gather.2.cloned.1.call-done), kind=kLoop, calls=%fused_computation.5 | loop fusion | bytes 75497472 | tf_op jit(solution)/shard_map/squeeze | solution.py:35
  163.9 15.2 %fusion.3 = f32[2,1,96,3072]{3,2,1,0:T(8,128)S(1)} fusion(bf16[1,3072,3072]{2,1,0:T(8,128)(2,1)} %get-tuple-element.6, bf16[1,3072,3072]{2,1,0:T(8,128)(2,1)} %get-tuple-element.5, bf16[1,1,96,6144]{3,2,0,1:T(8,128)(2,1)} %get-tuple-element.14, bf16[1,1,96,6144]{3,2,0,1:T(8,128)(2,1)} %get-tuple-element.13), kind=kOutput, calls=%fused_computation.6 | convolution fusion | flops 7327973376 | bytes 42467328 | tf_op jit(solution)/shard_map/cfik,fkn->cfin/dot_general | solution.py:36
  179.0 2.3 %fusion.7 = (f32[]{:T(128)}, f32[]{:T(128)}, f32[]{:T(128)}) fusion(f32[2,1,96,3072]{3,2,1,0:T(8,128)S(1)} %fusion.3, bf16[2,1,96,3072]{3,2,1,0:T(8,128)(2,1)S(1)} %copy-done), kind=kLoop, calls=%fused_computation.15 | loop fusion | flops 4718589 | bytes 3538956 | tf_op jit(solution)/shard_map/reduce_sum | solution.py:52
  181.3 2.1 pad_maximum_fusion.2
  183.4 12.0 %all_to_all.12 = f32[32,1,3]{2,1,0:T(1,128)S(1)} all-to-all(f32[32,1,3]{2,1,0:T(1,128)S(1)} %broadcast_in_dim.4), channel_id=1, replica_groups=mesh['freq'=4,'shot'=32] {'shot'}, dimensions={0} | all-to-all | bytes 768 | tf_op jit(solution)/shard_map/all_to_all | solution.py:13
  195.4 0.6 reduce_sum.48
  195.9 0.7 broadcast_in_dim.5
  196.6 7.9 %all_to_all.13 = f32[4,1,3]{2,1,0:T(1,128)S(1)} all-to-all(f32[4,1,3]{2,1,0:T(1,128)S(1)} %broadcast_in_dim.5), channel_id=1, replica_groups=mesh['freq'=4,'shot'=32] {'freq'}, dimensions={0} | all-to-all | bytes 96 | tf_op jit(solution)/shard_map/all_to_all | solution.py:13
  204.5 0.7 fusion.16
  207.3 0.6 subtract_convert_fusion.1
  207.9 1.6 pad_maximum_fusion
  (3 shorter events, 0.1 us)
Async XLA Ops:
  7.2 1.3 copy-start
  7.2 131.5 %all-gather.2.cloned.1.call-start = ((), (), s32[]{:S(2)}) async-start(), calls=%async_computation.2 | async-start | bytes 38928384 | tf_op jit(solution)/shard_map/all_gather | solution.py:45
Sparse Core Ops, SparseCore 0:
  10.3 128.3 all-gather.1
where the time goes:
time: 217 us; the launch traced here: 216 us
  waiting for transfers between devices  129 us (59%)
  local copies, waits for them, and re-layouts  27.1 us (12%)
  blocking collectives  19.9 us (9%)
  between operations  16.1 us (7%)
  matrix products  15.2 us (7%)
  other arithmetic  8.79 us (4%)
    all_gather x1, waiting for transfers between devices, per_device(): whole = lax.all_gather(traces, 'shot', axis=2, tiled=True)  129 us
    squeeze x1, local copies, waits for them, and re-layouts, complex_product(): right_block = jnp.concatenate([right[0], right[1]], axis=1)  25.2 us
    all_to_all x2, blocking collectives, from_everyone(): lax.all_to_all(jnp.broadcast_to(shard[None], (size, *shard.shape)), axis,...  19.9 us
    dot_general x1, matrix products, complex_product(): jnp.einsum('cfik,fkn->cfin', left_block, right_block, preferred_element_t...  15.2 us
  transfers between devices with their start and end apart: 1, of which 1 were waited for; matrix products, arithmetic and copies ran while one was open for 1% of the time, Pallas kernels for 0%

commit v1 on v0

v1 whole, which is shorter than its diff:
```python
import functools
import math

import jax
import jax.numpy as jnp
from jax import lax
from jax.experimental import pallas as pl
from jax.experimental.pallas import tpu as pltpu
from jax.sharding import PartitionSpec as P

epsilon = 1e-06
SIDE = 4
MESH = pl.DeviceIdType.MESH


def kernel(
    dims, x_ref, mult_ref, prim_ref,
    a, b, stage, prod, own, ostage, om, op, fita, fitb,
    local_sems,
    a_send, a_recv, b_send, b_recv, d_send, d_recv, o_send, o_recv,
    fa_send, fa_recv, fb_send, fb_recv,
):
    freqs, rows, order, width, chunks = dims
    block = order // SIDE
    scale = 1.0 / math.sqrt(order)
    f = lax.axis_index("freq")
    s = lax.axis_index("shot")
    c = lax.rem(s, 2)
    z = lax.rem(s // 2, SIDE)
    y = s // (2 * SIDE)
    p = z * (1 - c) + y * c
    q = y * (1 - c) + z * c

    def dev(qq, pp):
        return (1 - c) * ((qq * SIDE + pp) * 2) + c * ((pp * SIDE + qq) * 2 + 1)

    def turn(i, d):
        return lax.rem(i + d + SIDE, SIDE)

    sib = s + 1 - 2 * c
    pr, pl_, pfar = turn(p, 1), turn(p, -1), turn(p, 2)
    qr, ql, qfar = turn(q, 1), turn(q, -1), turn(q, 2)

    def cols(qq, pp, j):
        return pl.ds(pl.multiple_of(lax.rem(qq + pp, SIDE) * block + j * width, 128), width)

    def remote(src, dst, ss, rs, shot):
        return pltpu.make_async_remote_copy(
            src_ref=src, dst_ref=dst, send_sem=ss, recv_sem=rs,
            device_id={"shot": shot}, device_id_type=MESH,
        )

    load = pltpu.make_async_copy(x_ref, a.at[:, p], local_sems.at[0])
    load.start()

    barrier = pltpu.get_barrier_semaphore()
    partners = 0
    for i in range(SIDE):
        for k in range(SIDE):
            if i or k:
                pl.semaphore_signal(
                    barrier, inc=1, device_id={"shot": dev(turn(q, i), turn(p, k))}, device_id_type=MESH
                )
                partners += 1
    for i in range(freqs):
        for other in (0, 1):
            if i or other:
                pl.semaphore_signal(
                    barrier, inc=1,
                    device_id={"freq": lax.rem(f + i, freqs), "shot": sib if other else s},
                    device_id_type=MESH,
                )
                partners += 1
    pl.semaphore_wait(barrier, partners)
    load.wait()

    sent = []

    def go(copy):
        copy.start()
        sent.append(copy)
        return copy

    right, left = dev(q, pr), dev(q, pl_)
    ar = [go(remote(a.at[h, p], a.at[h, p], a_send.at[h], a_recv.at[h], right)) for h in (0, 1)]
    al = {h: go(remote(a.at[h, p], a.at[h, p], a_send.at[2 + h], a_recv.at[2 + h], left)) for h in (1, 0)}

    def from_left(h):
        return remote(a.at[h, pl_], a.at[h, pl_], a_send.at[h], a_recv.at[h], right)

    def from_right(h):
        return remote(a.at[h, pr], a.at[h, pr], a_send.at[2 + h], a_recv.at[2 + h], left)

    def far(h):
        return remote(a.at[h, pfar], a.at[h, pfar], a_send.at[4 + h], a_recv.at[4 + h], right)

    qright, qleft = dev(qr, p), dev(ql, p)
    ring = [p, pr, pl_, pfar]

    def b_own(j, r):
        pp = ring[r]
        return pltpu.make_async_copy(
            a.at[:, pp, :, cols(q, p, j)], b.at[j, :, dev(q, pp)], local_sems.at[1 + j * SIDE + r]
        )

    def b_dir(j, r, d):
        pp = ring[r]
        return remote(
            a.at[:, pp, :, cols(qr if d == 0 else ql, p, j)], b.at[j, :, dev(q, pp)],
            b_send.at[j, r, d], b_recv.at[j, r, d], qright if d == 0 else qleft,
        )

    def b_stage(j, r, h):
        pp = ring[r]
        return remote(
            a.at[h, pp, :, cols(qfar, p, j)], stage.at[j, h, r],
            b_send.at[j, r, 2 + h], b_recv.at[j, r, 2 + h], qright if h == 0 else qleft,
        )

    def b_fwd(j, r, h):
        pp = ring[r]
        return remote(
            stage.at[j, h, r], b.at[j, h, dev(ql if h == 0 else qr, pp)],
            b_send.at[j, r, 4 + h], b_recv.at[j, r, 4 + h], qright if h == 0 else qleft,
        )

    def d2d(j, r, k):
        kb = dev([q, qr, ql, qfar][k], ring[r])
        return remote(b.at[j, :, kb], b.at[j, :, kb], d_send.at[j, r, k], d_recv.at[j, r, k], sib)

    def d2d_src(j, r, k):
        sq, sp = p, q
        kk = turn(sq, [0, 1, -1, 2][k])
        rr = turn(sp, [0, 1, -1, 2][r])
        kb = c * ((kk * SIDE + rr) * 2) + (1 - c) * ((rr * SIDE + kk) * 2 + 1)
        return remote(b.at[j, :, kb], b.at[j, :, kb], d_send.at[j, r, k], d_recv.at[j, r, k], sib)

    locals_ = []

    def send_b(j, r):
        for h in (0, 1):
            go(b_stage(j, r, h))
        for d in (0, 1):
            go(b_dir(j, r, d))
        copy = b_own(j, r)
        copy.start()
        locals_.append(copy)

    def forward_b(j, r):
        for h in (0, 1):
            b_stage(j, r, h).wait_recv()
            go(b_fwd(j, r, h))

    send_b(0, 0)
    from_left(0).wait_recv()
    go(remote(a.at[0, pl_], a.at[0, pl_], a_send.at[4], a_recv.at[4], right))
    from_right(1).wait_recv()
    go(remote(a.at[1, pr], a.at[1, pr], a_send.at[5], a_recv.at[5], left))
    forward_b(0, 0)
    from_left(1).wait_recv()
    from_right(0).wait_recv()
    send_b(0, 1)
    send_b(0, 2)
    far(0).wait_recv()
    far(1).wait_recv()
    send_b(0, 3)
    for j in range(1, chunks):
        for r in range(SIDE):
            send_b(j, r)
    for r in range(1, SIDE):
        forward_b(0, r)

    def o_dir(j, d):
        return remote(
            prod.at[j, :, pr if d == 0 else pl_], own.at[:, :, cols(q, p, j)],
            o_send.at[j, d], o_recv.at[j, d], right if d == 0 else left,
        )

    def o_stage(j, h):
        return remote(
            prod.at[j, h, pfar], ostage.at[j, h],
            o_send.at[j, 2 + h], o_recv.at[j, 2 + h], right if h == 0 else left,
        )

    def o_fwd(j, h):
        return remote(
            ostage.at[j, h], own.at[h, :, cols(q, pl_ if h == 0 else pr, j)],
            o_send.at[j, 4 + h], o_recv.at[j, 4 + h], right if h == 0 else left,
        )

    def o_own(j):
        return pltpu.make_async_copy(
            prod.at[j, :, p], own.at[:, :, cols(q, p, j)], local_sems.at[1 + chunks * SIDE + j]
        )

    def forward_o(j):
        for h in (0, 1):
            o_stage(j, h).wait_recv()
            go(o_fwd(j, h))

    sums = [jnp.zeros((8, width), jnp.float32) for _ in range(3)]
    depth = SIDE * SIDE * 2 * rows
    for j in range(chunks):
        for r in range(SIDE):
            locals_[j * SIDE + r].wait()
            go(d2d(j, r, 0))
        for r in range(SIDE):
            for d in (0, 1):
                b_dir(j, r, d).wait_recv()
                go(d2d(j, r, 2 if d == 0 else 1))
        for r in range(SIDE):
            for h in (0, 1):
                b_fwd(j, r, h).wait_recv()
            go(d2d(j, r, 3))
        if j + 1 < chunks:
            for r in range(SIDE):
                forward_b(j + 1, r)
        for r in range(SIDE):
            for k in range(SIDE):
                d2d_src(j, r, k).wait_recv()
        here = cols(q, p, j)
        br = b[j, 0].reshape(depth, width)
        bi = b[j, 1].reshape(depth, width)
        for half in range(2):
            at = pl.ds(half * 2, 2)
            lhs = a[:, at].reshape(4 * rows, depth)
            xr = jnp.dot(lhs, br, preferred_element_type=jnp.float32)
            xi = jnp.dot(lhs, bi, preferred_element_type=jnp.float32)
            mr = (xr[: 2 * rows] - xi[2 * rows :]) * scale
            mi = (xi[: 2 * rows] + xr[2 * rows :]) * scale
            prod[j, 0, at] = mr.reshape(2, rows, width)
            prod[j, 1, at] = mi.reshape(2, rows, width)
            dr = a[0, at, :, here].reshape(2 * rows, width).astype(jnp.float32)
            di = a[1, at, :, here].reshape(2 * rows, width).astype(jnp.float32)
            terms = (mr * dr + mi * di, mr * di - mi * dr, mr * mr + mi * mi)
            sums = [u + jnp.sum(t.reshape(-1, 8, width), axis=0) for u, t in zip(sums, terms)]
        for h in (0, 1):
            go(o_stage(j, h))
        for d in (0, 1):
            go(o_dir(j, d))
        copy = o_own(j)
        copy.start()
        locals_.append(copy)
        if j:
            forward_o(j - 1)

    line = [jnp.sum(u.reshape(8, width // 128, 128).sum(axis=1), axis=0, keepdims=True) for u in sums]
    me = q * SIDE + p
    fita[me] = jnp.concatenate(line + [jnp.zeros((5, 128), jnp.float32)], axis=0)

    def fa(i, k, back=False):
        to = dev(turn(q, i), turn(p, k))
        slot = me if not back else turn(q, -i) * SIDE + turn(p, -k)
        n = i * SIDE + k
        return remote(fita.at[slot], fita.at[slot], fa_send.at[n], fa_recv.at[n], to)

    pairs = [(i, k) for i in range(SIDE) for k in range(SIDE) if i or k]
    for i, k in pairs:
        go(fa(i, k))
    forward_o(chunks - 1)
    for i, k in pairs:
        fa(i, k, True).wait_recv()
    group = jnp.sum(fita[...], axis=0)
    mine = f * 2 + c
    fitb[mine] = group

    def fb(i, other, back=False):
        cc = c if not other else 1 - c
        slot = mine if not back else lax.rem(f - i + freqs, freqs) * 2 + cc
        n = i * 2 + other
        return pltpu.make_async_remote_copy(
            src_ref=fitb.at[slot], dst_ref=fitb.at[slot], send_sem=fb_send.at[n], recv_sem=fb_recv.at[n],
            device_id={"freq": lax.rem(f + i, freqs), "shot": sib if other else s}, device_id_type=MESH,
        )

    others = [(i, o) for i in range(freqs) for o in (0, 1) if i or o]
    for i, o in others:
        go(fb(i, o))

    for j in range(chunks):
        locals_[chunks * SIDE + j].wait()
        for d in (0, 1):
            o_dir(j, d).wait_recv()
        for h in (0, 1):
            o_fwd(j, h).wait_recv()
    om[...] = own[...].astype(jnp.bfloat16)
    out_m = pltpu.make_async_copy(om, mult_ref, local_sems.at[0])
    out_m.start()

    for i, o in others:
        fb(i, o, True).wait_recv()
    total = jnp.sum(fitb[...], axis=0)
    total = jnp.sum(total, axis=1, keepdims=True)
    count = float(freqs * order * order)
    den = total[2:3] / count + epsilon
    fit_re = total[0:1] / count / den
    fit_im = total[1:2] / count / den
    for t in range(0, order, 512):
        at = pl.ds(t, 512)
        mr, mi = own[0, :, at], own[1, :, at]
        op[0, :, at] = (a[0, p, :, at].astype(jnp.float32) - (fit_re * mr - fit_im * mi)).astype(jnp.bfloat16)
        op[1, :, at] = (a[1, p, :, at].astype(jnp.float32) - (fit_re * mi + fit_im * mr)).astype(jnp.bfloat16)
    out_p = pltpu.make_async_copy(op, prim_ref, local_sems.at[1])
    out_p.start()
    for copy in sent:
        copy.wait_send()
    out_m.wait()
    out_p.wait()


def per_device(traces):
    rows, order = traces.shape[2], traces.shape[3]
    freqs = lax.axis_size("freq")
    block = order // SIDE
    width = 256 if block % 256 == 0 else 128
    chunks = block // width
    dma = pltpu.SemaphoreType.DMA
    out = jax.ShapeDtypeStruct((2, rows, order), jnp.bfloat16)
    shots = SIDE * SIDE * 2
    mult, prim = pl.pallas_call(
        functools.partial(kernel, (freqs, rows, order, width, chunks)),
        out_shape=(out, out),
        in_specs=[pl.BlockSpec(memory_space=pl.ANY)],
        out_specs=(pl.BlockSpec(memory_space=pl.ANY), pl.BlockSpec(memory_space=pl.ANY)),
        scratch_shapes=[
            pltpu.VMEM((2, SIDE, rows, order), jnp.bfloat16),
            pltpu.VMEM((chunks, 2, shots, rows, width), jnp.bfloat16),
            pltpu.VMEM((chunks, 2, SIDE, rows, width), jnp.bfloat16),
            pltpu.VMEM((chunks, 2, SIDE, rows, width), jnp.float32),
            pltpu.VMEM((2, rows, order), jnp.float32),
            pltpu.VMEM((chunks, 2, rows, width), jnp.float32),
            pltpu.VMEM((2, rows, order), jnp.bfloat16),
            pltpu.VMEM((2, rows, order), jnp.bfloat16),
            pltpu.VMEM((SIDE * SIDE, 8, 128), jnp.float32),
            pltpu.VMEM((freqs * 2, 8, 128), jnp.float32),
            dma((1 + chunks * SIDE + chunks,)),
            dma((6,)), dma((6,)),
            dma((chunks, SIDE, 6)), dma((chunks, SIDE, 6)),
            dma((chunks, SIDE, SIDE)), dma((chunks, SIDE, SIDE)),
            dma((chunks, 6)), dma((chunks, 6)),
            dma((SIDE * SIDE,)), dma((SIDE * SIDE,)),
            dma((freqs * 2,)), dma((freqs * 2,)),
        ],
        compiler_params=pltpu.CompilerParams(
            collective_id=0, has_side_effects=True, vmem_limit_bytes=60 * 1024 * 1024
        ),
    )(traces.reshape(2, rows, order))
    return mult.reshape(traces.shape), prim.reshape(traces.shape)


def solution(mesh):
    placed = P(None, "freq", "shot", None)
    return jax.shard_map(
        per_device,
        mesh=mesh,
        in_specs=(placed,),
        out_specs=(placed, placed),
        check_vma=False,
    )
```

time: 217 us -> 89.9 us (0.41)
  waiting for transfers between devices: 129 us -> 0 us
  Pallas kernels: 0 us -> 85.7 us
  local copies, waits for them, and re-layouts: 27.1 us -> 3.47 us
  blocking collectives: 19.9 us -> 0 us
  between operations: 16.1 us -> 0.65 us
  matrix products: 15.2 us -> 0 us
  other arithmetic: 8.79 us -> 0 us
    all_gather x1 -> x0, waiting for transfers between devices: 129 us -> none  [per_device(): whole = lax.all_gather(traces, 'shot', axis=2, tiled=True)]
    pallas_call x0 -> x1, Pallas kernels: none -> 85.7 us  [per_device(): pl.pallas_call(functools.partial(kernel, (freqs, rows, order, width, chun...]
    squeeze x2 -> x0, local copies, waits for them, and re-layouts: 25.3 us -> none  [the longest x1 25.2 us: complex_product(): right_block = jnp.concatenate([right[0], right[1]], axis=1)]
    all_to_all x2 -> x0, blocking collectives: 19.9 us -> none  [from_everyone(): lax.all_to_all(jnp.broadcast_to(shard[None], (size, *shard.shape)), axis,...]
    dot_general x1 -> x0, matrix products: 15.2 us -> none  [complex_product(): jnp.einsum('cfik,fkn->cfin', left_block, right_block, preferred_element_t...]
    another operation x3 -> x0, other arithmetic: 3.78 us -> none  [the longest x1 1.61 us: per_device(): multiples = jnp.stack([mult_re, mult_im]).astype(jnp.bfloat16)]
    unnamed x2 -> x4, local copies, waits for them, and re-layouts: 0.53 us -> 3.47 us
    reduce_sum x3 -> x0, other arithmetic: 2.91 us -> none  [the longest x1 2.33 us: per_device(): jnp.sum(mult_re * data_re + mult_im * data_im)]
  transfers between devices with their start and end apart: 1 -> 0, of which waited for: 1 -> 0; matrix products, arithmetic and copies ran while one was open for 1% -> 0% of each run, Pallas kernels for 0% -> 0%
where the time goes in v1:
time: 89.9 us; the launch traced here: 89.8 us
  Pallas kernels  85.7 us (95%)
  local copies, waits for them, and re-layouts  3.47 us (4%)
    pallas_call x1, Pallas kernels, per_device(): pl.pallas_call(functools.partial(kernel, (freqs, rows, order, width, chun...  85.7 us
    unnamed x4, local copies, waits for them, and re-layouts  3.47 us

profile of v1, /device:TPU:1, one launch (start us, length us, event | category | flops | bytes accessed | tf_op | source)
XLA Modules:
  0.0 89.8 jit_solution(3151471098604654392)
XLA Ops:
  0.6 85.7 %shard_map.30 = (bf16[2,96,3072]{2,1,0:T(8,128)(2,1)}, bf16[2,96,3072]{2,1,0:T(8,128)(2,1)}) custom-call(bf16[2,96,3072]{2,1,0:T(8,128)(2,1)} %bitcast.7), custom_call_target="tpu_custom_call" | custom-call | tf_op jit(solution)/shard_map/pallas_call | solution.py:320
  86.3 0.0 copy-start
  86.3 2.5 %copy.7 = bf16[2,1,96,3072]{3,2,1,0:T(8,128)(2,1)} copy(bf16[2,1,96,3072]{3,2,1,0:T(8,128)(2,1)} %bitcast.9) | data formatting | bytes 2359296
  88.8 0.0 copy-done
  88.8 1.0 %copy.8 = bf16[2,1,96,3072]{3,2,1,0:T(8,128)(2,1)} copy(bf16[2,1,96,3072]{3,2,1,0:T(8,128)(2,1)S(1)} %bitcast.8) | data formatting | bytes 2359296
Async XLA Ops:
  86.3 2.5 %copy-start = (bf16[2,96,3072]{2,1,0:T(8,128)(2,1)S(1)}, bf16[2,96,3072]{2,1,0:T(8,128)(2,1)}, u32[]{:S(2)}) copy-start(bf16[2,96,3072]{2,1,0:T(8,128)(2,1)} %get-tuple-element.5) | copy-start | bytes 3538948

commit v2 on v0

v2 whole, which is shorter than its diff:
```python
import functools
import math

import jax
import jax.numpy as jnp
from jax import lax
from jax.experimental import pallas as pl
from jax.experimental.pallas import tpu as pltpu
from jax.sharding import PartitionSpec as P

epsilon = 1e-06
SIDE = 4
MESH = pl.DeviceIdType.MESH
STEPS = (0, 1, -1, 2)


def kernel(dims, x_ref, mult_ref, prim_ref, *refs):
    freqs, rows, order, widths = dims
    chunks = len(widths)
    starts = [sum(widths[:j]) for j in range(chunks)]
    a, own, fit = refs[:3]
    b = refs[3 : 3 + chunks]
    prod = refs[3 + chunks : 3 + 2 * chunks]
    load_sem, own_sem, a_send, a_recv, b_send, b_recv, d_send, d_recv, o_send, o_recv, f_send, f_recv = refs[
        3 + 2 * chunks :
    ]
    block = order // SIDE
    scale = 1.0 / math.sqrt(order)
    f = lax.axis_index("freq")
    s = lax.axis_index("shot")
    c = lax.rem(s, 2)
    z = lax.rem(s // 2, SIDE)
    y = s // (2 * SIDE)
    p = z * (1 - c) + y * c
    q = y * (1 - c) + z * c

    def dev(qq, pp):
        return (1 - c) * ((qq * SIDE + pp) * 2) + c * ((pp * SIDE + qq) * 2 + 1)

    def turn(i, d):
        return lax.rem(i + d + SIDE, SIDE)

    sib = s + 1 - 2 * c
    ps = [turn(p, d) for d in STEPS]
    qs = [turn(q, d) for d in STEPS]
    pdev = [{"shot": dev(q, pp)} for pp in ps]
    qdev = [{"shot": dev(qq, p)} for qq in qs]
    xdev = [{"freq": lax.rem(f + i, freqs)} for i in range(freqs)]
    back = (0, 2, 1, 3)

    def cols(qq, pp, j):
        return pl.ds(pl.multiple_of(lax.rem(qq + pp, SIDE) * block + starts[j], 128), widths[j])

    def remote(src, dst, ss, rs, to):
        return pltpu.make_async_remote_copy(
            src_ref=src, dst_ref=dst, send_sem=ss, recv_sem=rs, device_id=to, device_id_type=MESH
        )

    load = pltpu.make_async_copy(x_ref, a.at[:, p], load_sem)
    load.start()

    barrier = pltpu.get_barrier_semaphore()
    near = pdev[1:] + qdev[1:] + [{"shot": sib}] + xdev[1:]
    for to in near:
        pl.semaphore_signal(barrier, inc=1, device_id=to, device_id_type=MESH)
    pl.semaphore_wait(barrier, len(near))
    load.wait()

    sent = []

    def go(copy):
        copy.start()
        sent.append(copy)
        return copy

    def a_copy(n, backward=False):
        h = (0, 1, 1, 0, 0, 1)[n]
        k = (0, 0, 0, 0, 2, 1)[n]
        to = (1, 1, 2, 2, 1, 2)[n]
        if backward:
            k = (2, 2, 1, 1, 3, 3)[n]
        here = a.at[h, ps[k]]
        return remote(here, here, a_send.at[n], a_recv.at[n], pdev[to])

    def b_own(j, r):
        return pltpu.make_async_copy(
            a.at[:, ps[r], :, cols(q, p, j)], b[j].at[:, dev(q, ps[r])], own_sem.at[j, r]
        )

    def b_copy(j, r, k):
        return remote(
            a.at[:, ps[r], :, cols(qs[k], p, j)], b[j].at[:, dev(q, ps[r])],
            b_send.at[j, r, k], b_recv.at[j, r, k], qdev[k],
        )

    def d_copy(j, r, k):
        kb = dev(qs[k], ps[r])
        here = b[j].at[:, kb]
        return remote(here, here, d_send.at[j, r, k], d_recv.at[j, r, k], {"shot": sib})

    def send_b(j, r):
        for k in (3, 1, 2):
            go(b_copy(j, r, k))
        b_own(j, r).start()

    for n in (0, 2, 1, 3):
        go(a_copy(n))
    send_b(0, 0)
    for n in (0, 2):
        a_copy(n, True).wait_recv()
        go(a_copy(n // 2 + 4))
    for n in (1, 3):
        a_copy(n, True).wait_recv()
    send_b(0, 1)
    send_b(0, 2)
    for n in (4, 5):
        a_copy(n, True).wait_recv()
    send_b(0, 3)
    for j in range(1, chunks):
        for r in range(SIDE):
            send_b(j, r)

    def o_copy(j, k):
        return remote(
            prod[j].at[:, ps[k]], own.at[:, :, cols(q, p, j)], o_send.at[j, k], o_recv.at[j, k], pdev[k]
        )

    def send_o(j):
        for k in (3, 1, 2):
            go(o_copy(j, k))

    sums = [jnp.zeros((8, 128), jnp.float32) for _ in range(3)]
    depth = SIDE * SIDE * 2 * rows
    for j in range(chunks):
        width = widths[j]
        for r in range(SIDE):
            b_own(j, r).wait()
            go(d_copy(j, r, 0))
        for r in range(SIDE):
            for k in (3, 1, 2):
                b_copy(j, r, k).wait_recv()
                go(d_copy(j, r, back[k]))
        if j == chunks - 1:
            for i in range(j):
                send_o(i)
        for r in range(SIDE):
            for k in range(SIDE):
                d_copy(j, r, k).wait_recv()
        here = cols(q, p, j)
        br = b[j][0].reshape(depth, width)
        bi = b[j][1].reshape(depth, width)
        for half in range(2):
            at = pl.ds(half * 2, 2)
            lhs = a[:, at].reshape(4 * rows, depth)
            if width == 128:
                x = jnp.dot(lhs, jnp.concatenate([br, bi], axis=1), preferred_element_type=jnp.float32)
                xr, xi = x[:, :128], x[:, 128:]
            else:
                xr = jnp.dot(lhs, br, preferred_element_type=jnp.float32)
                xi = jnp.dot(lhs, bi, preferred_element_type=jnp.float32)
            mr = (xr[: 2 * rows] - xi[2 * rows :]) * scale
            mi = (xi[: 2 * rows] + xr[2 * rows :]) * scale
            prod[j][0, at] = mr.reshape(2, rows, width)
            prod[j][1, at] = mi.reshape(2, rows, width)
            dr = a[0, at, :, here].reshape(2 * rows, width).astype(jnp.float32)
            di = a[1, at, :, here].reshape(2 * rows, width).astype(jnp.float32)
            terms = (mr * dr + mi * di, mr * di - mi * dr, mr * mr + mi * mi)
            for n, t in enumerate(terms):
                t = jnp.sum(t.reshape(-1, 8, width), axis=0)
                for w in range(0, width, 128):
                    sums[n] = sums[n] + t[:, w : w + 128]
    send_o(chunks - 1)

    line = [jnp.sum(u, axis=0, keepdims=True) for u in sums]
    value = jnp.concatenate(line + [jnp.zeros((5, 128), jnp.float32)], axis=0)
    stages = [
        (p, [pdev[1], pdev[3], pdev[2]], SIDE),
        (q, [qdev[1], qdev[3], qdev[2]], SIDE),
        (f, xdev[1:], freqs),
        (c, [{"shot": sib}], 2),
    ]
    for n, (me, to, size) in enumerate(stages):
        fit[n, me] = value

        def f_copy(i):
            here = fit.at[n, me]
            return remote(here, here, f_send.at[n, i], f_recv.at[n, i], to[i])

        def f_wait(i):
            there = fit.at[n, lax.rem(me - 1 - i + size, size)]
            return remote(there, there, f_send.at[n, i], f_recv.at[n, i], to[i])

        for i in range(size - 1):
            go(f_copy(i))
        for i in range(size - 1):
            f_wait(i).wait_recv()
        value = fit[n, 0]
        for i in range(1, size):
            value = value + fit[n, i]
    total = jnp.sum(value, axis=1, keepdims=True)
    count = float(freqs * order * order)
    den = total[2:3] / count + epsilon
    fit_re = total[0:1] / count / den
    fit_im = total[1:2] / count / den

    for j in range(chunks):
        for k in (0, 3, 1, 2):
            at = cols(q, ps[k], j)
            if k:
                o_copy(j, back[k]).wait_recv()
                mr, mi = own[0, :, at], own[1, :, at]
            else:
                mr, mi = prod[j][0, p], prod[j][1, p]
            mult_ref[0, :, at] = mr.astype(jnp.bfloat16)
            mult_ref[1, :, at] = mi.astype(jnp.bfloat16)
            dr, di = a[0, p, :, at].astype(jnp.float32), a[1, p, :, at].astype(jnp.float32)
            prim_ref[0, :, at] = (dr - (fit_re * mr - fit_im * mi)).astype(jnp.bfloat16)
            prim_ref[1, :, at] = (di - (fit_re * mi + fit_im * mr)).astype(jnp.bfloat16)
    for copy in sent:
        copy.wait_send()


def per_device(traces):
    rows, order = traces.shape[2], traces.shape[3]
    freqs = lax.axis_size("freq")
    widths = (256, 256, 256)
    chunks = len(widths)
    dma = pltpu.SemaphoreType.DMA
    out = jax.ShapeDtypeStruct((2, rows, order), jnp.bfloat16)
    shots = SIDE * SIDE * 2
    vmem = pl.BlockSpec(memory_space=pltpu.VMEM)
    mult, prim = pl.pallas_call(
        functools.partial(kernel, (freqs, rows, order, widths)),
        out_shape=(out, out),
        in_specs=[pl.BlockSpec(memory_space=pltpu.HBM)],
        out_specs=(vmem, vmem),
        scratch_shapes=[
            pltpu.VMEM((2, SIDE, rows, order), jnp.bfloat16),
            pltpu.VMEM((2, rows, order), jnp.float32),
            pltpu.VMEM((4, max(freqs, SIDE), 8, 128), jnp.float32),
            *[pltpu.VMEM((2, shots, rows, w), jnp.bfloat16) for w in widths],
            *[pltpu.VMEM((2, SIDE, rows, w), jnp.float32) for w in widths],
            dma, dma((chunks, SIDE)),
            dma((6,)), dma((6,)),
            dma((chunks, SIDE, SIDE)), dma((chunks, SIDE, SIDE)),
            dma((chunks, SIDE, SIDE)), dma((chunks, SIDE, SIDE)),
            dma((chunks, SIDE)), dma((chunks, SIDE)),
            dma((4, SIDE)), dma((4, SIDE)),
        ],
        compiler_params=pltpu.CompilerParams(
            collective_id=0, has_side_effects=True, vmem_limit_bytes=36 * 1024 * 1024
        ),
    )(pltpu.with_memory_space_constraint(traces.reshape(2, rows, order), pltpu.HBM))
    return mult.reshape(traces.shape), prim.reshape(traces.shape)


def solution(mesh):
    placed = P(None, "freq", "shot", None)
    return jax.shard_map(
        per_device,
        mesh=mesh,
        in_specs=(placed,),
        out_specs=(placed, placed),
        check_vma=False,
    )
```

time: 217 us -> 87 us (0.40)
  waiting for transfers between devices: 129 us -> 0 us
  Pallas kernels: 0 us -> 84.2 us
  local copies, waits for them, and re-layouts: 27.1 us -> 2.03 us
  blocking collectives: 19.9 us -> 0 us
  between operations: 16.1 us -> 0.64 us
  matrix products: 15.2 us -> 0 us
  other arithmetic: 8.79 us -> 0 us
    all_gather x1 -> x0, waiting for transfers between devices: 129 us -> none  [per_device(): whole = lax.all_gather(traces, 'shot', axis=2, tiled=True)]
    pallas_call x0 -> x1, Pallas kernels: none -> 84.2 us  [per_device(): pl.pallas_call(functools.partial(kernel, (freqs, rows, order, widths)), o...]
    squeeze x2 -> x0, local copies, waits for them, and re-layouts: 25.3 us -> none  [the longest x1 25.2 us: complex_product(): right_block = jnp.concatenate([right[0], right[1]], axis=1)]
    all_to_all x2 -> x0, blocking collectives: 19.9 us -> none  [from_everyone(): lax.all_to_all(jnp.broadcast_to(shard[None], (size, *shard.shape)), axis,...]
    dot_general x1 -> x0, matrix products: 15.2 us -> none  [complex_product(): jnp.einsum('cfik,fkn->cfin', left_block, right_block, preferred_element_t...]
    another operation x3 -> x0, other arithmetic: 3.78 us -> none  [the longest x1 1.61 us: per_device(): multiples = jnp.stack([mult_re, mult_im]).astype(jnp.bfloat16)]
    reduce_sum x3 -> x0, other arithmetic: 2.91 us -> none  [the longest x1 2.33 us: per_device(): jnp.sum(mult_re * data_re + mult_im * data_im)]
  transfers between devices with their start and end apart: 1 -> 0, of which waited for: 1 -> 0; matrix products, arithmetic and copies ran while one was open for 1% -> 0% of each run, Pallas kernels for 0% -> 0%
where the time goes in v2:
time: 87 us; the launch traced here: 86.9 us
  Pallas kernels  84.2 us (97%)
  local copies, waits for them, and re-layouts  2.03 us (2%)
    pallas_call x1, Pallas kernels, per_device(): pl.pallas_call(functools.partial(kernel, (freqs, rows, order, widths)), o...  84.2 us
    unnamed x2, local copies, waits for them, and re-layouts  2.03 us

profile of v2, /device:TPU:1, one launch (start us, length us, event | category | flops | bytes accessed | tf_op | source)
XLA Modules:
  0.0 86.9 jit_solution(12556846839871990341)
XLA Ops:
  0.6 84.2 %shard_map.30 = (bf16[2,96,3072]{2,1,0:T(8,128)(2,1)S(1)}, bf16[2,96,3072]{2,1,0:T(8,128)(2,1)S(1)}) custom-call(bf16[2,96,3072]{2,1,0:T(8,128)(2,1)} %bitcast.9), custom_call_target="tpu_custom_call" | custom-call | tf_op jit(solution)/shard_map/pallas_call | solution.py:232
  84.9 1.0 %copy.7 = bf16[2,1,96,3072]{3,2,1,0:T(8,128)(2,1)} copy(bf16[2,1,96,3072]{3,2,1,0:T(8,128)(2,1)S(1)} %bitcast.8) | data formatting | bytes 2359296
  85.9 1.0 %copy.8 = bf16[2,1,96,3072]{3,2,1,0:T(8,128)(2,1)} copy(bf16[2,1,96,3072]{3,2,1,0:T(8,128)(2,1)S(1)} %bitcast.7) | data formatting | bytes 2359296

commit v3 on v2

v3 whole, which is shorter than its diff:
```python
import functools
import math

import jax
import jax.numpy as jnp
from jax import lax
from jax.experimental import pallas as pl
from jax.experimental.pallas import tpu as pltpu
from jax.sharding import PartitionSpec as P

epsilon = 1e-06
SIDE = 4
MESH = pl.DeviceIdType.MESH
STEPS = (0, 1, -1, 2)


def kernel(
    dims, x_ref, mult_ref, prim_ref, a, b, prod, own, fit,
    load_sem, own_sem, a_send, a_recv, b_send, b_recv, d_send, d_recv, o_send, o_recv, f_send, f_recv,
):
    freqs, rows, order, widths = dims
    chunks = len(widths)
    starts = [sum(widths[:j]) for j in range(chunks)]
    block = order // SIDE
    scale = 1.0 / math.sqrt(order)
    f = lax.axis_index("freq")
    s = lax.axis_index("shot")
    c = lax.rem(s, 2)
    z = lax.rem(s // 2, SIDE)
    y = s // (2 * SIDE)
    p = z * (1 - c) + y * c
    q = y * (1 - c) + z * c

    def dev(qq, pp):
        return (1 - c) * ((qq * SIDE + pp) * 2) + c * ((pp * SIDE + qq) * 2 + 1)

    def turn(i, d):
        return lax.rem(i + d + SIDE, SIDE)

    ps = [turn(p, d) for d in STEPS]
    qs = [turn(q, d) for d in STEPS]
    pdev = [{"shot": dev(q, pp)} for pp in ps]
    qdev = [{"shot": dev(qq, p)} for qq in qs]
    xdev = [{"freq": lax.rem(f + i, freqs)} for i in range(freqs)]
    sib = {"shot": s + 1 - 2 * c}

    def lanes(j):
        return pl.ds(0, block) if j is None else pl.ds(starts[j], widths[j])

    def cols(qq, pp, j):
        at = lax.rem(qq + pp, SIDE) * block
        if j is None:
            return pl.ds(pl.multiple_of(at, 128), block)
        return pl.ds(pl.multiple_of(at + starts[j], 128), widths[j])

    def remote(src, dst, ss, rs, to):
        return pltpu.make_async_remote_copy(
            src_ref=src, dst_ref=dst, send_sem=ss, recv_sem=rs, device_id=to, device_id_type=MESH
        )

    def await_in(like, sem):
        remote(like, like, o_send, sem, sib).wait_recv()

    def await_out(like, sem):
        remote(like, like, sem, o_recv.at[0], sib).wait_send()

    load = pltpu.make_async_copy(x_ref, a.at[:, p], load_sem)
    load.start()

    barrier = pltpu.get_barrier_semaphore()
    near = pdev[1:] + qdev[1:] + [sib] + xdev[1:]
    for to in near:
        pl.semaphore_signal(barrier, inc=1, device_id=to, device_id_type=MESH)
    pl.semaphore_wait(barrier, len(near))
    load.wait()

    def send_a(n):
        h = (0, 1, 1, 0, 0, 1)[n]
        here = a.at[h, ps[(0, 0, 0, 0, 2, 1)[n]]]
        remote(here, here, a_send, a_recv.at[n], pdev[(1, 1, 2, 2, 1, 2)[n]]).start()

    def wait_a(n):
        await_in(a.at[(0, 1, 1, 0, 0, 1)[n], ps[(2, 2, 1, 1, 3, 3)[n]]], a_recv.at[n])

    def slot(r, j):
        return r if j is None else r + j

    def send_b(r, j=None):
        here = b.at[:, q * (1 - c) + ps[r] * c, ps[r] * (1 - c) + q * c, c, :, lanes(j)]
        for k in (3, 1, 2):
            remote(
                a.at[:, ps[r], :, cols(qs[k], p, j)], here, b_send, b_recv.at[slot(r, j)], qdev[k]
            ).start()
        pltpu.make_async_copy(a.at[:, ps[r], :, cols(q, p, j)], here, own_sem.at[slot(r, j)]).start()

    def pass_b(r, j=None):
        some = b.at[:, 0, :, 0, :, lanes(j)]
        mine = b.at[:, 0, 0, 0, :, lanes(j)]
        pltpu.make_async_copy(mine, mine, own_sem.at[slot(r, j)]).wait()
        await_in(b.at[:, 0, pl.ds(0, 3), 0, :, lanes(j)], b_recv.at[slot(r, j)])

        @pl.when(c == 0)
        def _():
            here = b.at[:, :, ps[r], 0, :, lanes(j)]
            remote(here, here, d_send, d_recv.at[slot(r, j)], sib).start()

        @pl.when(c == 1)
        def _():
            here = b.at[:, ps[r], :, 1, :, lanes(j)]
            remote(here, here, d_send, d_recv.at[slot(r, j)], sib).start()

        return some

    def wait_d(r, j=None):
        await_in(b.at[:, 0, :, 0, :, lanes(j)], d_recv.at[slot(r, j)])

    for n in (0, 2, 1, 3):
        send_a(n)
    send_b(0)
    for n in (0, 2):
        wait_a(n)
        send_a(n // 2 + 4)
    wait_a(1)
    send_b(2)
    wait_a(3)
    send_b(1)
    for n in (4, 5):
        wait_a(n)
    for j in range(chunks):
        send_b(3, j)
    for r in (0, 2, 1):
        pass_b(r)

    def send_o(j):
        for k in (3, 1, 2):
            remote(
                prod.at[:, ps[k], :, lanes(j)], own.at[:, :, cols(q, p, j)], o_send, o_recv.at[j], pdev[k]
            ).start()

    sums = [jnp.zeros((8, 128), jnp.float32) for _ in range(3)]
    depth = SIDE * SIDE * 2 * rows
    for j in range(chunks):
        width = widths[j]
        pass_b(3, j)
        if j == 0:
            for r in (0, 2, 1):
                wait_d(r)
        wait_d(3, j)
        here = cols(q, p, j)
        br = b[0, :, :, :, :, lanes(j)].reshape(depth, width)
        bi = b[1, :, :, :, :, lanes(j)].reshape(depth, width)
        for half in range(2):
            at = pl.ds(half * 2, 2)
            lhs = a[:, at].reshape(4 * rows, depth)
            if width == 128:
                x = jnp.dot(lhs, jnp.concatenate([br, bi], axis=1), preferred_element_type=jnp.float32)
                xr, xi = x[:, :128], x[:, 128:]
            else:
                xr = jnp.dot(lhs, br, preferred_element_type=jnp.float32)
                xi = jnp.dot(lhs, bi, preferred_element_type=jnp.float32)
            mr = (xr[: 2 * rows] - xi[2 * rows :]) * scale
            mi = (xi[: 2 * rows] + xr[2 * rows :]) * scale
            prod[0, at, :, lanes(j)] = mr.reshape(2, rows, width)
            prod[1, at, :, lanes(j)] = mi.reshape(2, rows, width)
            dr = a[0, at, :, here].reshape(2 * rows, width).astype(jnp.float32)
            di = a[1, at, :, here].reshape(2 * rows, width).astype(jnp.float32)
            terms = (mr * dr + mi * di, mr * di - mi * dr, mr * mr + mi * mi)
            for n, t in enumerate(terms):
                t = jnp.sum(t.reshape(-1, 8, width), axis=0)
                for w in range(0, width, 128):
                    sums[n] = sums[n] + t[:, w : w + 128]
        send_o(j)

    line = [jnp.sum(u, axis=0, keepdims=True) for u in sums]
    value = jnp.concatenate(line + [jnp.zeros((5, 128), jnp.float32)], axis=0)
    stages = [
        (c, [sib], 2),
        (f, xdev[1:], freqs),
        (q, [qdev[1], qdev[3], qdev[2]], SIDE),
        (p, [pdev[1], pdev[3], pdev[2]], SIDE),
    ]
    for n, (me, to, size) in enumerate(stages):
        fit[n, me] = value
        here = fit.at[n, me]
        for i in range(size - 1):
            remote(here, here, f_send.at[n], f_recv.at[n], to[i]).start()
        if size > 1:
            await_in(fit.at[n, pl.ds(0, size - 1)], f_recv.at[n])
        value = fit[n, 0]
        for i in range(1, size):
            value = value + fit[n, i]
    total = jnp.sum(value, axis=1, keepdims=True)
    count = float(freqs * order * order)
    den = total[2:3] / count + epsilon
    fit_re = total[0:1] / count / den
    fit_im = total[1:2] / count / den

    for j in range(chunks):
        for k in range(SIDE):
            at = cols(q, ps[k], j)
            if k:
                mr, mi = own[0, :, at], own[1, :, at]
            else:
                mr, mi = prod[0, p, :, lanes(j)], prod[1, p, :, lanes(j)]
            mult_ref[0, :, at] = mr.astype(jnp.bfloat16)
            mult_ref[1, :, at] = mi.astype(jnp.bfloat16)
            dr, di = a[0, p, :, at].astype(jnp.float32), a[1, p, :, at].astype(jnp.float32)
            prim_ref[0, :, at] = (dr - (fit_re * mr - fit_im * mi)).astype(jnp.bfloat16)
            prim_ref[1, :, at] = (di - (fit_re * mi + fit_im * mr)).astype(jnp.bfloat16)
            if k == 0:
                await_in(prod.at[:, pl.ds(0, 3), :, lanes(j)], o_recv.at[j])
    await_out(a.at[:, pl.ds(0, 3)], a_send)
    await_out(b.at[:, pl.ds(0, 3), :, 0], b_send)
    await_out(b.at[:, :, :, 0], d_send)
    await_out(prod.at[:, pl.ds(0, 3)], o_send)
    for n, (_, _, size) in enumerate(stages):
        if size > 1:
            await_out(fit.at[n, pl.ds(0, size - 1)], f_send.at[n])


def per_device(traces):
    rows, order = traces.shape[2], traces.shape[3]
    freqs = lax.axis_size("freq")
    block = order // SIDE
    widths = (256, 256, 256)
    chunks = len(widths)
    dma = pltpu.SemaphoreType.DMA
    out = jax.ShapeDtypeStruct((2, rows, order), jnp.bfloat16)
    vmem = pl.BlockSpec(memory_space=pltpu.VMEM)
    mult, prim = pl.pallas_call(
        functools.partial(kernel, (freqs, rows, order, widths)),
        out_shape=(out, out),
        in_specs=[pl.BlockSpec(memory_space=pltpu.HBM)],
        out_specs=(vmem, vmem),
        scratch_shapes=[
            pltpu.VMEM((2, SIDE, rows, order), jnp.bfloat16),
            pltpu.VMEM((2, SIDE, SIDE, 2, rows, block), jnp.bfloat16),
            pltpu.VMEM((2, SIDE, rows, block), jnp.float32),
            pltpu.VMEM((2, rows, order), jnp.float32),
            pltpu.VMEM((4, max(freqs, SIDE), 8, 128), jnp.float32),
            dma, dma((3 + chunks,)),
            dma, dma((6,)),
            dma, dma((3 + chunks,)),
            dma, dma((3 + chunks,)),
            dma, dma((chunks,)),
            dma((4,)), dma((4,)),
        ],
        compiler_params=pltpu.CompilerParams(
            collective_id=0, has_side_effects=True, vmem_limit_bytes=36 * 1024 * 1024
        ),
    )(pltpu.with_memory_space_constraint(traces.reshape(2, rows, order), pltpu.HBM))
    return mult.reshape(traces.shape), prim.reshape(traces.shape)


def solution(mesh):
    placed = P(None, "freq", "shot", None)
    return jax.shard_map(
        per_device,
        mesh=mesh,
        in_specs=(placed,),
        out_specs=(placed, placed),
        check_vma=False,
    )
```

time: 87 us -> 78.1 us (0.90)
  the two profiles are of different devices: /device:TPU:1 before, /device:TPU:0 now
where the time goes in v3:
time: 78.1 us; the launch traced here: 78 us
  Pallas kernels  75.3 us (96%)
  local copies, waits for them, and re-layouts  2.03 us (3%)
    pallas_call x1, Pallas kernels, per_device(): pl.pallas_call(functools.partial(kernel, (freqs, rows, order, widths)), o...  75.3 us
    unnamed x2, local copies, waits for them, and re-layouts  2.03 us

profile of v3, /device:TPU:0, one launch (start us, length us, event | category | flops | bytes accessed | tf_op | source)
XLA Modules:
  0.0 78.0 jit_solution(11102151184120937872)
XLA Ops:
  0.6 75.3 %shard_map.30 = (bf16[2,96,3072]{2,1,0:T(8,128)(2,1)S(1)}, bf16[2,96,3072]{2,1,0:T(8,128)(2,1)S(1)}) custom-call(bf16[2,96,3072]{2,1,0:T(8,128)(2,1)} %bitcast.9), custom_call_target="tpu_custom_call" | custom-call | tf_op jit(solution)/shard_map/pallas_call | solution.py:230
  76.0 1.0 %copy.7 = bf16[2,1,96,3072]{3,2,1,0:T(8,128)(2,1)} copy(bf16[2,1,96,3072]{3,2,1,0:T(8,128)(2,1)S(1)} %bitcast.8) | data formatting | bytes 2359296
  77.0 1.0 %copy.8 = bf16[2,1,96,3072]{3,2,1,0:T(8,128)(2,1)} copy(bf16[2,1,96,3072]{3,2,1,0:T(8,128)(2,1)S(1)} %bitcast.7) | data formatting | bytes 2359296

commit v4 on v3

--- a/solution.py
+++ b/solution.py
@@ -18,7 +18,8 @@
     dims, x_ref, mult_ref, prim_ref, a, b, prod, own, fit,
     load_sem, own_sem, a_send, a_recv, b_send, b_recv, d_send, d_recv, o_send, o_recv, f_send, f_recv,
 ):
-    freqs, rows, order, widths = dims
+    freqs, rows, order, widths, plan = dims
+    pieces = [piece for part in plan for piece in part]
     chunks = len(widths)
     starts = [sum(widths[:j]) for j in range(chunks)]
     block = order // SIDE
@@ -44,14 +45,16 @@
     xdev = [{"freq": lax.rem(f + i, freqs)} for i in range(freqs)]
     sib = {"shot": s + 1 - 2 * c}
 
-    def lanes(j):
-        return pl.ds(0, block) if j is None else pl.ds(starts[j], widths[j])
-
-    def cols(qq, pp, j):
-        at = lax.rem(qq + pp, SIDE) * block
-        if j is None:
-            return pl.ds(pl.multiple_of(at, 128), block)
-        return pl.ds(pl.multiple_of(at + starts[j], 128), widths[j])
+    ends = starts[1:] + [block]
+
+    def lanes(i, j=None):
+        j = i if j is None else j
+        return pl.ds(starts[i], ends[j] - starts[i])
+
+    def cols(qq, pp, i, j=None):
+        j = i if j is None else j
+        at = lax.rem(qq + pp, SIDE) * block + starts[i]
+        return pl.ds(pl.multiple_of(at, 128), ends[j] - starts[i])
 
     def remote(src, dst, ss, rs, to):
         return pltpu.make_async_remote_copy(
@@ -82,54 +85,49 @@
     def wait_a(n):
         await_in(a.at[(0, 1, 1, 0, 0, 1)[n], ps[(2, 2, 1, 1, 3, 3)[n]]], a_recv.at[n])
 
-    def slot(r, j):
-        return r if j is None else r + j
-
-    def send_b(r, j=None):
-        here = b.at[:, q * (1 - c) + ps[r] * c, ps[r] * (1 - c) + q * c, c, :, lanes(j)]
-        for k in (3, 1, 2):
-            remote(
-                a.at[:, ps[r], :, cols(qs[k], p, j)], here, b_send, b_recv.at[slot(r, j)], qdev[k]
-            ).start()
-        pltpu.make_async_copy(a.at[:, ps[r], :, cols(q, p, j)], here, own_sem.at[slot(r, j)]).start()
-
-    def pass_b(r, j=None):
-        some = b.at[:, 0, :, 0, :, lanes(j)]
-        mine = b.at[:, 0, 0, 0, :, lanes(j)]
-        pltpu.make_async_copy(mine, mine, own_sem.at[slot(r, j)]).wait()
-        await_in(b.at[:, 0, pl.ds(0, 3), 0, :, lanes(j)], b_recv.at[slot(r, j)])
+    def send_b(piece):
+        n = pieces.index(piece)
+        r, lo, hi = piece
+        here = b.at[:, q * (1 - c) + ps[r] * c, ps[r] * (1 - c) + q * c, c, :, lanes(lo, hi)]
+        for k in (1, 2, 3):
+            remote(a.at[:, ps[r], :, cols(qs[k], p, lo, hi)], here, b_send, b_recv.at[n], qdev[k]).start()
+        pltpu.make_async_copy(a.at[:, ps[r], :, cols(q, p, lo, hi)], here, own_sem.at[n]).start()
+
+    def pass_b(piece):
+        n = pieces.index(piece)
+        r, lo, hi = piece
+        mine = b.at[:, 0, 0, 0, :, lanes(lo, hi)]
+        pltpu.make_async_copy(mine, mine, own_sem.at[n]).wait()
+        await_in(b.at[:, 0, pl.ds(0, 3), 0, :, lanes(lo, hi)], b_recv.at[n])
 
         @pl.when(c == 0)
         def _():
-            here = b.at[:, :, ps[r], 0, :, lanes(j)]
-            remote(here, here, d_send, d_recv.at[slot(r, j)], sib).start()
+            here = b.at[:, :, ps[r], 0, :, lanes(lo, hi)]
+            remote(here, here, d_send, d_recv.at[n], sib).start()
 
         @pl.when(c == 1)
         def _():
-            here = b.at[:, ps[r], :, 1, :, lanes(j)]
-            remote(here, here, d_send, d_recv.at[slot(r, j)], sib).start()
-
-        return some
-
-    def wait_d(r, j=None):
-        await_in(b.at[:, 0, :, 0, :, lanes(j)], d_recv.at[slot(r, j)])
+            here = b.at[:, ps[r], :, 1, :, lanes(lo, hi)]
+            remote(here, here, d_send, d_recv.at[n], sib).start()
+
+    def wait_d(piece):
+        await_in(b.at[:, 0, :, 0, :, lanes(*piece[1:])], d_recv.at[pieces.index(piece)])
 
     for n in (0, 2, 1, 3):
         send_a(n)
-    send_b(0)
+    for piece in plan[0]:
+        send_b(piece)
     for n in (0, 2):
         wait_a(n)
         send_a(n // 2 + 4)
-    wait_a(1)
-    send_b(2)
-    wait_a(3)
-    send_b(1)
+    for n in (1, 3):
+        wait_a(n)
+    for piece in plan[1]:
+        send_b(piece)
     for n in (4, 5):
         wait_a(n)
-    for j in range(chunks):
-        send_b(3, j)
-    for r in (0, 2, 1):
-        pass_b(r)
+    for piece in plan[2]:
+        send_b(piece)
 
     def send_o(j):
         for k in (3, 1, 2):
@@ -139,13 +137,15 @@
 
     sums = [jnp.zeros((8, 128), jnp.float32) for _ in range(3)]
     depth = SIDE * SIDE * 2 * rows
+    passed = 0
     for j in range(chunks):
         width = widths[j]
-        pass_b(3, j)
-        if j == 0:
-            for r in (0, 2, 1):
-                wait_d(r)
-        wait_d(3, j)
+        last = max(n for n, (r, lo, hi) in enumerate(pieces) if lo <= j)
+        for piece in pieces[passed : last + 1]:
+            pass_b(piece)
+        for piece in pieces[passed : last + 1]:
+            wait_d(piece)
+        passed = max(passed, last + 1)
         here = cols(q, p, j)
         br = b[0, :, :, :, :, lanes(j)].reshape(depth, width)
         bi = b[1, :, :, :, :, lanes(j)].reshape(depth, width)
@@ -224,11 +224,13 @@
     block = order // SIDE
     widths = (256, 256, 256)
     chunks = len(widths)
+    plan = ((), ((0, 0, 2), (2, 0, 1), (1, 0, 1)), ((3, 0, 0), (3, 1, 1), (2, 2, 2), (1, 2, 2), (3, 2, 2)))
+    pieces = sum(len(part) for part in plan)
     dma = pltpu.SemaphoreType.DMA
     out = jax.ShapeDtypeStruct((2, rows, order), jnp.bfloat16)
     vmem = pl.BlockSpec(memory_space=pltpu.VMEM)
     mult, prim = pl.pallas_call(
-        functools.partial(kernel, (freqs, rows, order, widths)),
+        functools.partial(kernel, (freqs, rows, order, widths, plan)),
         out_shape=(out, out),
         in_specs=[pl.BlockSpec(memory_space=pltpu.HBM)],
         out_specs=(vmem, vmem),
@@ -238,10 +240,10 @@
             pltpu.VMEM((2, SIDE, rows, block), jnp.float32),
             pltpu.VMEM((2, rows, order), jnp.float32),
             pltpu.VMEM((4, max(freqs, SIDE), 8, 128), jnp.float32),
-            dma, dma((3 + chunks,)),
+            dma, dma((pieces,)),
             dma, dma((6,)),
-            dma, dma((3 + chunks,)),
-            dma, dma((3 + chunks,)),
+            dma, dma((pieces,)),
+            dma, dma((pieces,)),
             dma, dma((chunks,)),
             dma((4,)), dma((4,)),
         ],

time: 78.1 us -> 74.7 us (0.956)
  the two profiles are of different devices: /device:TPU:0 before, /device:TPU:1 now
where the time goes in v4:
time: 74.7 us; the launch traced here: 74.1 us
  Pallas kernels  71.5 us (96%)
  local copies, waits for them, and re-layouts  2.03 us (3%)
    pallas_call x1, Pallas kernels, per_device(): pl.pallas_call(functools.partial(kernel, (freqs, rows, order, widths, pla...  71.5 us
    unnamed x2, local copies, waits for them, and re-layouts  2.03 us

profile of v4, /device:TPU:1, one launch (start us, length us, event | category | flops | bytes accessed | tf_op | source)
XLA Modules:
  0.0 74.1 jit_solution(15815321831134830074)
XLA Ops:
  0.6 71.5 %shard_map.30 = (bf16[2,96,3072]{2,1,0:T(8,128)(2,1)S(1)}, bf16[2,96,3072]{2,1,0:T(8,128)(2,1)S(1)}) custom-call(bf16[2,96,3072]{2,1,0:T(8,128)(2,1)} %bitcast.9), custom_call_target="tpu_custom_call" | custom-call | tf_op jit(solution)/shard_map/pallas_call | solution.py:232
  72.1 1.0 %copy.7 = bf16[2,1,96,3072]{3,2,1,0:T(8,128)(2,1)} copy(bf16[2,1,96,3072]{3,2,1,0:T(8,128)(2,1)S(1)} %bitcast.8) | data formatting | bytes 2359296
  73.1 1.0 %copy.8 = bf16[2,1,96,3072]{3,2,1,0:T(8,128)(2,1)} copy(bf16[2,1,96,3072]{3,2,1,0:T(8,128)(2,1)S(1)} %bitcast.7) | data formatting | bytes 2359296

commit v5 on v4

--- a/solution.py
+++ b/solution.py
@@ -15,7 +15,7 @@
 
 
 def kernel(
-    dims, x_ref, mult_ref, prim_ref, a, b, prod, own, fit,
+    dims, x_ref, own, fit_ref, a, b, prod, fit, plane,
     load_sem, own_sem, a_send, a_recv, b_send, b_recv, d_send, d_recv, o_send, o_recv, f_send, f_recv,
 ):
     freqs, rows, order, widths, plan = dims
@@ -42,7 +42,6 @@
     qs = [turn(q, d) for d in STEPS]
     pdev = [{"shot": dev(q, pp)} for pp in ps]
     qdev = [{"shot": dev(qq, p)} for qq in qs]
-    xdev = [{"freq": lax.rem(f + i, freqs)} for i in range(freqs)]
     sib = {"shot": s + 1 - 2 * c}
 
     ends = starts[1:] + [block]
@@ -71,7 +70,9 @@
     load.start()
 
     barrier = pltpu.get_barrier_semaphore()
-    near = pdev[1:] + qdev[1:] + [sib] + xdev[1:]
+    ids = [(i, k) for i in range(freqs) for k in (0, 1) if i or k]
+    fdev = [{"freq": lax.rem(f + i, freqs), "shot": s + k * (1 - 2 * c)} for i, k in ids]
+    near = pdev[1:] + qdev[1:] + fdev
     for to in near:
         pl.semaphore_signal(barrier, inc=1, device_id=to, device_id_type=MESH)
     pl.semaphore_wait(barrier, len(near))
@@ -172,50 +173,51 @@
         send_o(j)
 
     line = [jnp.sum(u, axis=0, keepdims=True) for u in sums]
-    value = jnp.concatenate(line + [jnp.zeros((5, 128), jnp.float32)], axis=0)
-    stages = [
-        (c, [sib], 2),
-        (f, xdev[1:], freqs),
-        (q, [qdev[1], qdev[3], qdev[2]], SIDE),
-        (p, [pdev[1], pdev[3], pdev[2]], SIDE),
-    ]
-    for n, (me, to, size) in enumerate(stages):
-        fit[n, me] = value
-        here = fit.at[n, me]
-        for i in range(size - 1):
-            remote(here, here, f_send.at[n], f_recv.at[n], to[i]).start()
-        if size > 1:
-            await_in(fit.at[n, pl.ds(0, size - 1)], f_recv.at[n])
-        value = fit[n, 0]
-        for i in range(1, size):
-            value = value + fit[n, i]
-    total = jnp.sum(value, axis=1, keepdims=True)
-    count = float(freqs * order * order)
-    den = total[2:3] / count + epsilon
-    fit_re = total[0:1] / count / den
-    fit_im = total[1:2] / count / den
-
+    mine = fit.at[f * 2 + c]
+    mine[...] = jnp.concatenate(line + [jnp.zeros((5, 128), jnp.float32)], axis=0)
+    for to in fdev:
+        remote(mine, mine, f_send.at[0], f_recv.at[0], to).start()
     for j in range(chunks):
-        for k in range(SIDE):
-            at = cols(q, ps[k], j)
-            if k:
-                mr, mi = own[0, :, at], own[1, :, at]
-            else:
-                mr, mi = prod[0, p, :, lanes(j)], prod[1, p, :, lanes(j)]
-            mult_ref[0, :, at] = mr.astype(jnp.bfloat16)
-            mult_ref[1, :, at] = mi.astype(jnp.bfloat16)
-            dr, di = a[0, p, :, at].astype(jnp.float32), a[1, p, :, at].astype(jnp.float32)
-            prim_ref[0, :, at] = (dr - (fit_re * mr - fit_im * mi)).astype(jnp.bfloat16)
-            prim_ref[1, :, at] = (di - (fit_re * mi + fit_im * mr)).astype(jnp.bfloat16)
-            if k == 0:
-                await_in(prod.at[:, pl.ds(0, 3), :, lanes(j)], o_recv.at[j])
+        own[:, :, cols(q, p, j)] = prod[:, p, :, lanes(j)]
+    await_in(fit.at[pl.ds(0, len(fdev))], f_recv.at[0])
+    here = plane.at[q * SIDE + p]
+    here[...] = jnp.sum(fit[...], axis=0)
+    others = [(i, k) for i in range(SIDE) for k in range(SIDE) if i or k]
+    for i, k in others:
+        remote(here, here, f_send.at[1], f_recv.at[1], {"shot": dev(qs[i], ps[k])}).start()
+    for j in range(chunks):
+        await_in(prod.at[:, pl.ds(0, 3), :, lanes(j)], o_recv.at[j])
+    await_in(plane.at[pl.ds(0, len(others))], f_recv.at[1])
+    fit_ref[...] = jnp.sum(plane[...], axis=0)
     await_out(a.at[:, pl.ds(0, 3)], a_send)
     await_out(b.at[:, pl.ds(0, 3), :, 0], b_send)
     await_out(b.at[:, :, :, 0], d_send)
     await_out(prod.at[:, pl.ds(0, 3)], o_send)
-    for n, (_, _, size) in enumerate(stages):
-        if size > 1:
-            await_out(fit.at[n, pl.ds(0, size - 1)], f_send.at[n])
+    await_out(fit.at[pl.ds(0, len(fdev))], f_send.at[0])
+    await_out(plane.at[pl.ds(0, len(others))], f_send.at[1])
+
+
+def finish(count, own, fit, x, mult_ref, prim_ref, mult, prim, m_sem, p_sem):
+    total = jnp.sum(fit[...], axis=1, keepdims=True)
+    den = total[2:3] / count + epsilon
+    fit_re = total[0:1] / count / den
+    fit_im = total[1:2] / count / den
+    rows = own.shape[1]
+    copies = []
+    for n in range(rows // 32):
+        at = pl.ds(n * 32, 32)
+        mr, mi = own[0, at], own[1, at]
+        mult[0, at] = mr.astype(jnp.bfloat16)
+        mult[1, at] = mi.astype(jnp.bfloat16)
+        copies.append(pltpu.make_async_copy(mult.at[:, at], mult_ref.at[:, at], m_sem.at[n]))
+        copies[-1].start()
+        dr, di = x[0, at].astype(jnp.float32), x[1, at].astype(jnp.float32)
+        prim[0, at] = (dr - (fit_re * mr - fit_im * mi)).astype(jnp.bfloat16)
+        prim[1, at] = (di - (fit_re * mi + fit_im * mr)).astype(jnp.bfloat16)
+        copies.append(pltpu.make_async_copy(prim.at[:, at], prim_ref.at[:, at], p_sem.at[n]))
+        copies[-1].start()
+    for copy in copies:
+        copy.wait()
 
 
 def per_device(traces):
@@ -229,28 +231,45 @@
     dma = pltpu.SemaphoreType.DMA
     out = jax.ShapeDtypeStruct((2, rows, order), jnp.bfloat16)
     vmem = pl.BlockSpec(memory_space=pltpu.VMEM)
-    mult, prim = pl.pallas_call(
+    x = traces.reshape(2, rows, order)
+    anywhere = pl.BlockSpec(memory_space=pl.ANY)
+    own, fit = pl.pallas_call(
         functools.partial(kernel, (freqs, rows, order, widths, plan)),
-        out_shape=(out, out),
+        out_shape=(
+            jax.ShapeDtypeStruct((2, rows, order), jnp.float32),
+            jax.ShapeDtypeStruct((8, 128), jnp.float32),
+        ),
         in_specs=[pl.BlockSpec(memory_space=pltpu.HBM)],
         out_specs=(vmem, vmem),
         scratch_shapes=[
             pltpu.VMEM((2, SIDE, rows, order), jnp.bfloat16),
             pltpu.VMEM((2, SIDE, SIDE, 2, rows, block), jnp.bfloat16),
             pltpu.VMEM((2, SIDE, rows, block), jnp.float32),
-            pltpu.VMEM((2, rows, order), jnp.float32),
-            pltpu.VMEM((4, max(freqs, SIDE), 8, 128), jnp.float32),
+            pltpu.VMEM((freqs * 2, 8, 128), jnp.float32),
+            pltpu.VMEM((SIDE * SIDE, 8, 128), jnp.float32),
             dma, dma((pieces,)),
             dma, dma((6,)),
             dma, dma((pieces,)),
             dma, dma((pieces,)),
             dma, dma((chunks,)),
-            dma((4,)), dma((4,)),
+            dma((2,)), dma((2,)),
         ],
         compiler_params=pltpu.CompilerParams(
             collective_id=0, has_side_effects=True, vmem_limit_bytes=36 * 1024 * 1024
         ),
-    )(pltpu.with_memory_space_constraint(traces.reshape(2, rows, order), pltpu.HBM))
+    )(pltpu.with_memory_space_constraint(x, pltpu.HBM))
+    mult, prim = pl.pallas_call(
+        functools.partial(finish, float(freqs * order * order)),
+        out_shape=(out, out),
+        in_specs=[vmem, vmem, vmem],
+        out_specs=(anywhere, anywhere),
+        scratch_shapes=[
+            pltpu.VMEM((2, rows, order), jnp.bfloat16),
+            pltpu.VMEM((2, rows, order), jnp.bfloat16),
+            dma((rows // 32,)), dma((rows // 32,)),
+        ],
+        compiler_params=pltpu.CompilerParams(vmem_limit_bytes=16 * 1024 * 1024),
+    )(own, fit, x)
     return mult.reshape(traces.shape), prim.reshape(traces.shape)
 
 

time: 74.7 us -> 72.3 us (0.968)
  local copies, waits for them, and re-layouts: 2.03 us -> 0.01 us
    unnamed x2, local copies, waits for them, and re-layouts: 2.03 us -> 0.01 us
    pallas_call x0 -> x1, Pallas kernels: none -> 1.85 us  [per_device(): pl.pallas_call(functools.partial(finish, float(freqs * order * order)), o...]
    pallas_call x1, Pallas kernels: 71.5 us -> 69.7 us  [per_device(): pl.pallas_call(functools.partial(kernel, (freqs, rows, order, widths, pla...]
where the time goes in v5:
time: 72.3 us; the launch traced here: 72.2 us
  Pallas kernels  71.5 us (99%)
    pallas_call x1, Pallas kernels, per_device(): pl.pallas_call(functools.partial(kernel, (freqs, rows, order, widths, pla...  69.7 us
    pallas_call x1, Pallas kernels, per_device(): pl.pallas_call(functools.partial(finish, float(freqs * order * order)), o...  1.85 us

profile of v5, /device:TPU:1, one launch (start us, length us, event | category | flops | bytes accessed | tf_op | source)
XLA Modules:
  0.0 72.2 jit_solution(4312913523427818137)
XLA Ops:
  0.6 0.0 copy-start
  0.6 69.7 %shard_map.30 = (f32[2,96,3072]{2,1,0:T(8,128)S(1)}, f32[8,128]{1,0:T(8,128)S(1)}) custom-call(bf16[2,96,3072]{2,1,0:T(8,128)(2,1)} %bitcast.7), custom_call_target="tpu_custom_call" | custom-call | tf_op jit(solution)/shard_map/pallas_call | solution.py:236
  70.3 0.0 copy-done
  70.3 1.9 %shard_map.31 = (bf16[2,96,3072]{2,1,0:T(8,128)(2,1)}, bf16[2,96,3072]{2,1,0:T(8,128)(2,1)}) custom-call(f32[2,96,3072]{2,1,0:T(8,128)S(1)} %get-tuple-element.6.own, f32[8,128]{1,0:T(8,128)S(1)} %get-tuple-element.7.fit, bf16[2,96,3072]{2,1,0:T(8,128)(2,1)S(1)} %bitcast.8), custom_call_target="tpu_custom_call" | custom-call | tf_op jit(solution)/shard_map/pallas_call | solution.py:261
Async XLA Ops:
  0.6 69.7 %copy-start = (bf16[2,1,96,3072]{3,2,1,0:T(8,128)(2,1)S(1)}, bf16[2,1,96,3072]{3,2,1,0:T(8,128)(2,1)}, u32[]{:S(2)}) copy-start(bf16[2,1,96,3072]{3,2,1,0:T(8,128)(2,1)} %param.1) | copy-start | bytes 3538948

commit v6 on v5

--- a/solution.py
+++ b/solution.py
@@ -170,13 +170,15 @@
                 t = jnp.sum(t.reshape(-1, 8, width), axis=0)
                 for w in range(0, width, 128):
                     sums[n] = sums[n] + t[:, w : w + 128]
-        send_o(j)
+        if j < chunks - 1:
+            send_o(j)
 
     line = [jnp.sum(u, axis=0, keepdims=True) for u in sums]
     mine = fit.at[f * 2 + c]
     mine[...] = jnp.concatenate(line + [jnp.zeros((5, 128), jnp.float32)], axis=0)
     for to in fdev:
         remote(mine, mine, f_send.at[0], f_recv.at[0], to).start()
+    send_o(chunks - 1)
     for j in range(chunks):
         own[:, :, cols(q, p, j)] = prod[:, p, :, lanes(j)]
     await_in(fit.at[pl.ds(0, len(fdev))], f_recv.at[0])
@@ -204,8 +206,8 @@
     fit_im = total[1:2] / count / den
     rows = own.shape[1]
     copies = []
-    for n in range(rows // 32):
-        at = pl.ds(n * 32, 32)
+    for n in range(rows // 16):
+        at = pl.ds(n * 16, 16)
         mr, mi = own[0, at], own[1, at]
         mult[0, at] = mr.astype(jnp.bfloat16)
         mult[1, at] = mi.astype(jnp.bfloat16)
@@ -266,7 +268,7 @@
         scratch_shapes=[
             pltpu.VMEM((2, rows, order), jnp.bfloat16),
             pltpu.VMEM((2, rows, order), jnp.bfloat16),
-            dma((rows // 32,)), dma((rows // 32,)),
+            dma((rows // 16,)), dma((rows // 16,)),
         ],
         compiler_params=pltpu.CompilerParams(vmem_limit_bytes=16 * 1024 * 1024),
     )(own, fit, x)

time: 72.3 us -> 72.2 us (level)
  no operation moved by 1% of the time
where the time goes in v6:
time: 72.2 us; the launch traced here: 72.1 us
  Pallas kernels  71.4 us (99%)
    pallas_call x1, Pallas kernels, per_device(): pl.pallas_call(functools.partial(kernel, (freqs, rows, order, widths, pla...  69.8 us
    pallas_call x1, Pallas kernels, per_device(): pl.pallas_call(functools.partial(finish, float(freqs * order * order)), o...  1.68 us

profile of v6, /device:TPU:1, one launch (start us, length us, event | category | flops | bytes accessed | tf_op | source)
XLA Modules:
  0.0 72.1 jit_solution(2770159217655547599)
XLA Ops:
  0.6 0.0 copy-start
  0.6 69.8 %shard_map.30 = (f32[2,96,3072]{2,1,0:T(8,128)S(1)}, f32[8,128]{1,0:T(8,128)S(1)}) custom-call(bf16[2,96,3072]{2,1,0:T(8,128)(2,1)} %bitcast.7), custom_call_target="tpu_custom_call" | custom-call | tf_op jit(solution)/shard_map/pallas_call | solution.py:238
  70.4 0.0 copy-done
  70.4 1.7 %shard_map.31 = (bf16[2,96,3072]{2,1,0:T(8,128)(2,1)}, bf16[2,96,3072]{2,1,0:T(8,128)(2,1)}) custom-call(f32[2,96,3072]{2,1,0:T(8,128)S(1)} %get-tuple-element.6.own, f32[8,128]{1,0:T(8,128)S(1)} %get-tuple-element.7.fit, bf16[2,96,3072]{2,1,0:T(8,128)(2,1)S(1)} %bitcast.8), custom_call_target="tpu_custom_call" | custom-call | tf_op jit(solution)/shard_map/pallas_call | solution.py:263
Async XLA Ops:
  0.6 69.8 %copy-start = (bf16[2,1,96,3072]{3,2,1,0:T(8,128)(2,1)S(1)}, bf16[2,1,96,3072]{3,2,1,0:T(8,128)(2,1)}, u32[]{:S(2)}) copy-start(bf16[2,1,96,3072]{3,2,1,0:T(8,128)(2,1)} %param.1) | copy-start | bytes 3538948

commit v7 on v6

--- a/solution.py
+++ b/solution.py
@@ -187,9 +187,9 @@
     others = [(i, k) for i in range(SIDE) for k in range(SIDE) if i or k]
     for i, k in others:
         remote(here, here, f_send.at[1], f_recv.at[1], {"shot": dev(qs[i], ps[k])}).start()
+    await_in(plane.at[pl.ds(0, len(others))], f_recv.at[1])
     for j in range(chunks):
         await_in(prod.at[:, pl.ds(0, 3), :, lanes(j)], o_recv.at[j])
-    await_in(plane.at[pl.ds(0, len(others))], f_recv.at[1])
     fit_ref[...] = jnp.sum(plane[...], axis=0)
     await_out(a.at[:, pl.ds(0, 3)], a_send)
     await_out(b.at[:, pl.ds(0, 3), :, 0], b_send)

time: 72.2 us -> 72.2 us (level)
  no operation moved by 1% of the time
where the time goes in v7:
time: 72.2 us; the launch traced here: 72.1 us
  Pallas kernels  71.4 us (99%)
    pallas_call x1, Pallas kernels, per_device(): pl.pallas_call(functools.partial(kernel, (freqs, rows, order, widths, pla...  69.8 us
    pallas_call x1, Pallas kernels, per_device(): pl.pallas_call(functools.partial(finish, float(freqs * order * order)), o...  1.68 us

profile of v7, /device:TPU:1, one launch (start us, length us, event | category | flops | bytes accessed | tf_op | source)
XLA Modules:
  0.0 72.1 jit_solution(13621473357371419215)
XLA Ops:
  0.6 0.0 copy-start
  0.6 69.8 %shard_map.30 = (f32[2,96,3072]{2,1,0:T(8,128)S(1)}, f32[8,128]{1,0:T(8,128)S(1)}) custom-call(bf16[2,96,3072]{2,1,0:T(8,128)(2,1)} %bitcast.7), custom_call_target="tpu_custom_call" | custom-call | tf_op jit(solution)/shard_map/pallas_call | solution.py:238
  70.4 0.0 copy-done
  70.4 1.7 %shard_map.31 = (bf16[2,96,3072]{2,1,0:T(8,128)(2,1)}, bf16[2,96,3072]{2,1,0:T(8,128)(2,1)}) custom-call(f32[2,96,3072]{2,1,0:T(8,128)S(1)} %get-tuple-element.6.own, f32[8,128]{1,0:T(8,128)S(1)} %get-tuple-element.7.fit, bf16[2,96,3072]{2,1,0:T(8,128)(2,1)S(1)} %bitcast.8), custom_call_target="tpu_custom_call" | custom-call | tf_op jit(solution)/shard_map/pallas_call | solution.py:263
Async XLA Ops:
  0.6 69.8 %copy-start = (bf16[2,1,96,3072]{3,2,1,0:T(8,128)(2,1)S(1)}, bf16[2,1,96,3072]{3,2,1,0:T(8,128)(2,1)}, u32[]{:S(2)}) copy-start(bf16[2,1,96,3072]{3,2,1,0:T(8,128)(2,1)} %param.1) | copy-start | bytes 3538948
